TPU v7x, 32 devices: a whole 2x2x4 slice. The times are simulated.
32 devices in a mesh: parts: 2 (over y), modes: 16 (over z, x, core).
Axes of the slice: x: 2, y: 2, z: 4, core: 2. Of those that a mesh axis runs over, the one named last changes fastest.
Arguments:
- stem: bfloat16 [2, 16, 64, 32, 512], P(None, 'modes', None, None, 'parts'), parts along dimension 4, may hold values from -6 to 6
- branch_one: bfloat16 [2, 1024, 1024], replicated, may hold values from -0.125 to 0.125
- branch_two: bfloat16 [2, 1024, 1024], replicated, may hold values from -0.125 to 0.125
- branch_three: bfloat16 [2, 2, 16, 512, 512], P(None, None, 'modes'), may hold values from -0.0625 to 0.0625
- leg_orders: int32 [2, 10], replicated, may hold values from 0 to 9, each once within a row
- slice_pick: int32 [32], P('parts'), parts along dimension 0, may hold values from 0 to 1
Outputs:
- contracted: bfloat16 [1024, 2, 2, 2, 256], P(('parts', 'modes')), parts along dimension 0
There are 2 independent parts, one for each index of `parts`. A program takes and returns all parts, laid end to end along the dimension named above; an argument that names none is the same for every part. Nothing has to cross between parts.
Inputs may be any that keep to these rules, and one draw needn't show every extreme that they name: `leg_orders`: each row names every input leg bit once.
All inputs are finite; a program needn't handle non-finite values.
Results may differ from a plain program's by a relative error of at most 0.008.
Values may be sent and summed in bfloat16 or wider, within the bound.
A program may use at most 128 MiB of HBM per device.

v0:
```python
import jax
import jax.numpy as jnp
from jax import lax
from jax.experimental import pallas as pl
from jax.experimental.pallas import tpu as pltpu
from jax.sharding import PartitionSpec as P

TILES = 4


def leg_index(order, leg_width):
    positions = jnp.arange(leg_width, dtype=jnp.int32)
    shifts = jnp.arange(order.shape[0], dtype=jnp.int32)
    digits = jnp.right_shift(positions[:, None], shifts[None, :]) % 2
    placed = jnp.left_shift(digits, order[None, :])
    return jnp.sum(placed, axis=1)


def turned(branch, order):
    width = branch.shape[2]
    source = leg_index(order, width)
    rows = lax.broadcasted_iota(jnp.int32, (width, width), 0)
    onehot = (rows == source[None, :]).astype(branch.dtype)
    flat = branch.reshape(-1, width)
    out = jnp.dot(flat, onehot, preferred_element_type=jnp.float32)
    return out.astype(branch.dtype).reshape(branch.shape)


def complex_tile(w, values):
    half = values.shape[1] // 2
    p = jnp.dot(w[0], values, preferred_element_type=jnp.float32)
    q = jnp.dot(w[1], values, preferred_element_type=jnp.float32)
    real = p[:, :half] - q[:, half:]
    imag = p[:, half:] + q[:, :half]
    return real.astype(jnp.bfloat16), imag.astype(jnp.bfloat16)


def two_branches(x_hbm, w1_hbm, w2_hbm, out, x, w1, w2, mid, sems):
    width = x.shape[0]
    half = width // 2
    tile = width // TILES
    lanes = x.shape[1] // 8
    copies = [pltpu.make_async_copy(x_hbm, x, sems.at[0])]
    for which, (source, target) in enumerate(((w1_hbm, w1), (w2_hbm, w2))):
        for i in range(TILES):
            rows = pl.ds(i * tile, tile)
            copies.append(
                pltpu.make_async_copy(
                    source.at[:, rows, :], target.at[:, rows, :], sems.at[1 + which * TILES + i]
                )
            )
    for copy in copies:
        copy.start()
    copies[0].wait()
    for i in range(TILES):
        copies[1 + i].wait()
        t, c = divmod(i * tile, half)
        parts = complex_tile(w1[:, i * tile : (i + 1) * tile, :], x[...])
        for r in range(2):
            for a in range(2):
                at = (2 * r + t) * 2 * lanes
                mid[a * half + c : a * half + c + tile, at : at + 2 * lanes] = parts[r][
                    :, a * 2 * lanes : (a + 1) * 2 * lanes
                ]
    for i in range(TILES):
        copies[1 + TILES + i].wait()
        u, c = divmod(i * tile, half)
        parts = complex_tile(w2[:, i * tile : (i + 1) * tile, :], mid[...])
        for r in range(2):
            for td in range(4):
                at = (2 * r + u) * lanes
                out[td, c : c + tile, at : at + lanes] = parts[r][:, td * lanes : (td + 1) * lanes]


def third_branch(place, wa, wb, wc, wd, values, out):
    k2 = place[0]
    k0 = place[1]
    half = values.shape[2] // 2
    p = q = None
    for w, t, d in ((wa, k2, k0), (wb, 1 - k2, k0), (wc, k2, 1 - k0), (wd, 1 - k2, 1 - k0)):
        block = values[2 * t + d]
        pp = jnp.dot(w[0], block, preferred_element_type=jnp.float32)
        qq = jnp.dot(w[1], block, preferred_element_type=jnp.float32)
        p = pp if p is None else p + pp
        q = qq if q is None else q + qq
    out[:, :half] = (p[:, :half] - q[:, half:]).astype(out.dtype)
    out[:, half:] = (p[:, half:] + q[:, :half]).astype(out.dtype)


def per_device(stem, branch_one, branch_two, branch_three, leg_orders, slice_pick):
    groups = lax.axis_size("modes")
    me = lax.axis_index("modes")
    rest = groups // 8
    entries, lanes = stem.shape[2], stem.shape[4] // 2
    k2 = (me // (2 * rest)) % 2
    quarter = me // (2 * rest)
    k0 = me % 2

    cut = stem.reshape(2, entries, 2, 2, rest, 2, 2, 2, lanes)
    cut = cut.transpose(3, 7, 4, 5, 1, 0, 2, 6, 8).reshape(groups, entries, 8 * lanes)
    arrived = lax.all_to_all(cut, "modes", split_axis=0, concat_axis=0, tiled=True)
    x = arrived.reshape(groups * entries, 8 * lanes)

    pick = lax.dynamic_index_in_dim(slice_pick, me, 0, keepdims=False)
    own = lax.dynamic_index_in_dim(branch_three, pick, 0, keepdims=False)[:, 0]
    q = 2 * rest
    middle = [(q + i, 2 * q + i) for i in range(q)]
    middle += [(b, a) for a, b in middle]
    outer = [(i, i ^ q) for i in range(groups)] if q & (q - 1) == 0 else [
        (i, i + q if (i // q) % 2 == 0 else i - q) for i in range(groups)
    ]
    cores = [(i, i ^ 1) for i in range(groups)]
    crossed = lax.ppermute(own, "modes", middle)
    inner = (quarter == 1) | (quarter == 2)
    wa = jnp.where(inner, crossed, own)
    wb = lax.ppermute(wa, "modes", outer)
    wc = lax.ppermute(wa, "modes", cores)
    wd = lax.ppermute(wb, "modes", cores)

    w1 = turned(branch_one, leg_orders[0])
    w2 = turned(branch_two, leg_orders[1])
    width = w1.shape[1]
    half = width // 2
    any_spec = pl.BlockSpec(memory_space=pl.ANY)
    vmem = pl.BlockSpec(memory_space=pltpu.VMEM)
    values = pl.pallas_call(
        two_branches,
        name="two_branches",
        out_shape=jax.ShapeDtypeStruct((4, half, 4 * lanes), jnp.bfloat16),
        in_specs=[any_spec] * 3,
        out_specs=vmem,
        scratch_shapes=[
            pltpu.VMEM(x.shape, x.dtype),
            pltpu.VMEM(w1.shape, w1.dtype),
            pltpu.VMEM(w2.shape, w2.dtype),
            pltpu.VMEM((width, 8 * lanes), jnp.bfloat16),
            pltpu.SemaphoreType.DMA((1 + 2 * TILES,)),
        ],
        compiler_params=pltpu.CompilerParams(vmem_limit_bytes=40 * 2**20),
        cost_estimate=pl.CostEstimate(
            flops=8 * width * width * 8 * lanes, bytes_accessed=12 * 2**20, transcendentals=0
        ),
    )(x, w1, w2)

    out_width = own.shape[1]
    partial = pl.pallas_call(
        third_branch,
        name="third_branch",
        out_shape=jax.ShapeDtypeStruct((out_width, 4 * lanes), jnp.bfloat16),
        in_specs=[pl.BlockSpec(memory_space=pltpu.SMEM)] + [vmem] * 5,
        out_specs=vmem,
        compiler_params=pltpu.CompilerParams(vmem_limit_bytes=24 * 2**20),
        cost_estimate=pl.CostEstimate(
            flops=16 * out_width * half * 4 * lanes, bytes_accessed=7 * 2**20, transcendentals=0
        ),
    )(jnp.stack([k2, k0]).astype(jnp.int32), wa, wb, wc, wd, values)

    pieces = lax.all_to_all(partial, "modes", split_axis=0, concat_axis=0, tiled=True)
    mine = out_width // groups
    pieces = pieces.reshape(2, 2, rest, 2, mine, 2, 2, lanes).astype(jnp.float32)
    summed = jnp.sum(pieces, axis=(0, 2)).astype(jnp.bfloat16)
    return summed.transpose(2, 3, 4, 1, 0, 5).reshape(mine, 2, 2, 2, 2 * lanes)


def solution(mesh):
    in_specs = (
        P(None, "modes", None, None, "parts"),
        P(),
        P(),
        P(None, None, "modes", None, None),
        P(),
        P("parts"),
    )
    out_specs = P(("parts", "modes"), None, None, None, None)
    return jax.shard_map(
        per_device, mesh=mesh, in_specs=in_specs, out_specs=out_specs, check_vma=False
    )
```

profile of v0, /device:TPU:0, one launch (start us, length us, event | category | flops | bytes accessed | tf_op | source)
XLA Modules:
  0.0 173.0 jit_solution(10615352808761466327)
XLA Ops:
  0.0 4.0 %reshape.33 = bf16[2,64,2,2,2,2,2,2,128]{8,7,6,5,4,3,2,1,0:T(2,128)(2,1)} reshape(bf16[2,1,64,32,256]{4,3,2,1,0:T(8,128)(2,1)} %param.6) | data formatting | bytes 4194304 | tf_op jit(solution)/shard_map/reshape | solution.py:99
  4.0 3.1 %copy.18 = bf16[2,2,2,2,64,2,2,2,128]{8,7,6,5,4,3,2,1,0:T(2,128)(2,1)S(1)} copy(bf16[2,2,2,2,64,2,2,2,128]{8,1,7,3,2,0,6,4,5:T(2,128)(2,1)} %bitcast.31) | data formatting | bytes 4194304 | tf_op jit(solution)/shard_map/transpose | solution.py:100
  7.0 0.0 copy-start.4
  7.0 2.7 %reshape.34 = bf16[16,64,1024]{2,1,0:T(8,128)(2,1)} reshape(bf16[2,2,2,2,64,2,2,2,128]{8,7,6,5,4,3,2,1,0:T(2,128)(2,1)S(1)} %copy.18) | data formatting | bytes 4194304 | tf_op jit(solution)/shard_map/reshape | solution.py:100
  9.8 0.0 copy-start.2
  9.8 7.5 %all-to-all-start = ((bf16[16,64,1024]{2,1,0:T(8,128)(2,1)}), bf16[16,64,1024]{2,1,0:T(8,128)(2,1)S(1)}, u32[]{:S(2)}, u32[]{:S(2)}) async-start(bf16[16,64,1024]{2,1,0:T(8,128)(2,1)} %reshape.34), calls=%async_computation | async-start | bytes 4194304 | tf_op jit(solution)/shard_map/all_to_all | solution.py:101
  17.3 0.0 copy-done.4
  17.3 0.6 dynamic_slice.8
  19.9 1.3 dynamic-slice_bitcast_fusion
  21.2 1.6 collective-permute-start
  22.8 0.0 collective-permute-done
  22.8 1.3 broadcast_select_fusion.wa
  24.1 67.1 %collective-permute-start.1 = (bf16[2,512,512]{2,1,0:T(8,128)(2,1)S(1)}, bf16[2,512,512]{2,1,0:T(8,128)(2,1)}, u32[]{:S(2)}, u32[]{:S(2)}) collective-permute-start(bf16[2,512,512]{2,1,0:T(8,128)(2,1)S(1)} %broadcast_select_fusion.wa), channel_id=1, source_target_pairs={{0,4},{1,5},{2,6},{3,7},{4,0},{5,1},{6,2},{7,3},{8,12},{9,13},{10,... | collective-permute-start | bytes 3145736 | tf_op jit(solution)/shard_map/ppermute | solution.py:116
  91.2 0.0 copy-done.2
  91.2 0.1 shift-left_reduce_fusion
  91.3 0.0 copy-start.3
  91.3 8.5 %convert_bitcast_fusion = bf16[2048,1024]{0,1:T(8,128)(2,1)} fusion(bf16[2048,1024]{1,0:T(8,128)(2,1)} %bitcast.33, s32[1024]{0:T(1024)S(1)} %get-tuple-element.7), kind=kOutput, calls=%fused_computation | convolution fusion | flops 4299161600 | bytes 8392704 | tf_op jit(solution)/shard_map/dot_general | solution.py:25
  99.8 0.0 collective-permute-start.2
  99.8 14.3 %collective-permute-done.1.wb = bf16[2,512,512]{2,1,0:T(8,128)(2,1)} collective-permute-done((bf16[2,512,512]{2,1,0:T(8,128)(2,1)S(1)}, bf16[2,512,512]{2,1,0:T(8,128)(2,1)}, u32[]{:S(2)}, u32[]{:S(2)}) %collective-permute-start.1) | collective-permute-done | bytes 1048608 | tf_op jit(solution)/shard_map/ppermute | solution.py:116
  114.2 0.0 collective-permute-start.3
  114.2 0.0 copy-done.3
  114.2 6.2 %convert_bitcast_fusion.1 = bf16[2048,1024]{0,1:T(8,128)(2,1)} fusion(bf16[2048,1024]{1,0:T(8,128)(2,1)S(1)} %bitcast.34, s32[1024]{0:T(1024)S(1)} %get-tuple-element.8), kind=kOutput, calls=%fused_computation.2 | convolution fusion | flops 4299161600 | bytes 8392704 | tf_op jit(solution)/shard_map/dot_general | solution.py:25
  120.4 6.4 %copy.20 = bf16[2048,1024]{1,0:T(8,128)(2,1)} copy(bf16[2048,1024]{0,1:T(8,128)(2,1)} %convert_bitcast_fusion) | data formatting | bytes 8388608 | tf_op jit(solution)/shard_map/convert_element_type | solution.py:26
  126.8 6.4 %copy.19 = bf16[2048,1024]{1,0:T(8,128)(2,1)} copy(bf16[2048,1024]{0,1:T(8,128)(2,1)} %convert_bitcast_fusion.1) | data formatting | bytes 8388608 | tf_op jit(solution)/shard_map/convert_element_type | solution.py:26
  133.2 0.1 pad_add_fusion.place
  133.3 0.0 all-to-all-done
  133.3 0.0 copy-start
  133.3 2.2 %copy-done = bf16[2048,1024]{1,0:T(8,128)(2,1)S(1)} copy-done((bf16[2048,1024]{1,0:T(8,128)(2,1)S(1)}, bf16[2048,1024]{1,0:T(8,128)(2,1)}, u32[]{:S(2)}) %copy-start) | copy-done | bytes 4194328
  135.5 0.0 copy-start.1
  135.5 2.2 %copy-done.1 = bf16[2048,1024]{1,0:T(8,128)(2,1)S(1)} copy-done((bf16[2048,1024]{1,0:T(8,128)(2,1)S(1)}, bf16[2048,1024]{1,0:T(8,128)(2,1)}, u32[]{:S(2)}) %copy-start.1) | copy-done | bytes 4194328
  137.7 11.1 %two_branches.1.values = bf16[4,512,512]{2,1,0:T(8,128)(2,1)S(1)} custom-call(bf16[1024,1024]{1,0:T(8,128)(2,1)S(1)} %bitcast.29, bf16[2,1024,1024]{2,1,0:T(8,128)(2,1)S(1)} %bitcast.28, bf16[2,1024,1024]{2,1,0:T(8,128)(2,1)S(1)} %bitcast.27), custom_call_target="tpu_custom_call" | custom-call | flops 8589934592 | bytes 12582912 | tf_op jit(solution)/shard_map/two_branches/pallas_call | solution.py:126
  148.7 0.0 collective-permute-done.2.wc
  148.7 0.0 collective-permute-done.3.wd
  148.7 4.2 %third_branch.1 = bf16[512,512]{1,0:T(8,128)(2,1)S(1)} custom-call(s32[2]{0:T(128)S(1)} %pad_add_fusion.place, bf16[2,512,512]{2,1,0:T(8,128)(2,1)S(1)} %broadcast_select_fusion.wa, bf16[2,512,512]{2,1,0:T(8,128)(2,1)} %collective-permute-done.1.wb, bf16[2,512,512]{2,1,0:T(8,128)(2,1)} %collective-permute-done.2.wc, ...), custom_call_target="tpu_custom_call" | custom-call | flops 2147483648 | bytes 7340032 | tf_op jit(solution)/shard_map/third_branch/pallas_call | solution.py:146
  152.9 18.3 %all_to_all.14 = bf16[16,32,512]{2,1,0:T(8,128)(2,1)S(1)} all-to-all(bf16[16,32,512]{2,1,0:T(8,128)(2,1)S(1)} %bitcast.30), channel_id=1, replica_groups=mesh['parts'=2,'modes'=16] {'modes'}, dimensions={0} | all-to-all | bytes 1048576 | tf_op jit(solution)/shard_map/all_to_all | solution.py:158
  171.2 0.1 reshape.40
  171.3 0.8 reduce_sum.32
  172.1 0.1 copy.23
  172.3 0.7 reshape.42
  (1 shorter events, 0.0 us)
Async XLA Ops:
  7.0 10.3 %copy-start.4 = (s32[16]{0:T(128)S(1)}, s32[16]{0:T(128)}, u32[]{:S(2)}) copy-start(s32[16]{0:T(128)} %param.11) | copy-start | bytes 196
  9.8 81.4 %copy-start.2 = (s32[2,10]{1,0:T(2,128)S(1)}, s32[2,10]{1,0:T(2,128)}, u32[]{:S(2)}) copy-start(s32[2,10]{1,0:T(2,128)} %param.10) | copy-start | bytes 244
  9.8 123.5 %all-to-all-start = ((bf16[16,64,1024]{2,1,0:T(8,128)(2,1)}), bf16[16,64,1024]{2,1,0:T(8,128)(2,1)S(1)}, u32[]{:S(2)}, u32[]{:S(2)}) async-start(bf16[16,64,1024]{2,1,0:T(8,128)(2,1)} %reshape.34), calls=%async_computation | async-start | bytes 4194304 | tf_op jit(solution)/shard_map/all_to_all | solution.py:101
  21.2 1.6 collective-permute-start
  24.1 90.0 %collective-permute-start.1 = (bf16[2,512,512]{2,1,0:T(8,128)(2,1)S(1)}, bf16[2,512,512]{2,1,0:T(8,128)(2,1)}, u32[]{:S(2)}, u32[]{:S(2)}) collective-permute-start(bf16[2,512,512]{2,1,0:T(8,128)(2,1)S(1)} %broadcast_select_fusion.wa), channel_id=1, source_target_pairs={{0,4},{1,5},{2,6},{3,7},{4,0},{5,1},{6,2},{7,3},{8,12},{9,13},{10,... | collective-permute-start | bytes 3145736 | tf_op jit(solution)/shard_map/ppermute | solution.py:116
  91.3 22.9 %copy-start.3 = (bf16[2,1024,1024]{2,1,0:T(8,128)(2,1)S(1)}, bf16[2,1024,1024]{2,1,0:T(8,128)(2,1)}, u32[]{:S(2)}) copy-start(bf16[2,1024,1024]{2,1,0:T(8,128)(2,1)} %param.7) | copy-start | bytes 12582916
  99.8 48.9 %collective-permute-start.2 = (bf16[2,512,512]{2,1,0:T(8,128)(2,1)S(1)}, bf16[2,512,512]{2,1,0:T(8,128)(2,1)}, u32[]{:S(2)}, u32[]{:S(2)}) collective-permute-start(bf16[2,512,512]{2,1,0:T(8,128)(2,1)S(1)} %broadcast_select_fusion.wa), channel_id=1, source_target_pairs={{0,1},{1,0},{2,3},{3,2},{4,5},{5,4},{6,7},{7,6},{8,9},{9,8},{10,11... | collective-permute-start | bytes 3145736 | tf_op jit(solution)/shard_map/ppermute | solution.py:117
  114.2 34.6 %collective-permute-start.3 = (bf16[2,512,512]{2,1,0:T(8,128)(2,1)}, bf16[2,512,512]{2,1,0:T(8,128)(2,1)}, u32[]{:S(2)}, u32[]{:S(2)}) collective-permute-start(bf16[2,512,512]{2,1,0:T(8,128)(2,1)} %collective-permute-done.1.wb), channel_id=1, source_target_pairs={{0,1},{1,0},{2,3},{3,2},{4,5},{5,4},{6,7},{7,6},{8,9},{9,8},{10,11... | collective-permute-start | bytes 3145736 | tf_op jit(solution)/shard_map/ppermute | solution.py:118
  133.3 2.2 %copy-start = (bf16[2048,1024]{1,0:T(8,128)(2,1)S(1)}, bf16[2048,1024]{1,0:T(8,128)(2,1)}, u32[]{:S(2)}) copy-start(bf16[2048,1024]{1,0:T(8,128)(2,1)} %copy.20) | copy-start | bytes 12582916
  135.5 2.2 %copy-start.1 = (bf16[2048,1024]{1,0:T(8,128)(2,1)S(1)}, bf16[2048,1024]{1,0:T(8,128)(2,1)}, u32[]{:S(2)}) copy-start(bf16[2048,1024]{1,0:T(8,128)(2,1)} %copy.19) | copy-start | bytes 12582916
where the time goes:
time: 174 us; the launch traced here: 173 us
  starting transfers between devices  76.2 us (44%)
  local copies, waits for them, and re-layouts  29.9 us (17%)
  blocking collectives  18.3 us (11%)
  Pallas kernels  15.3 us (9%)
  matrix products  14.7 us (8%)
  waiting for transfers between devices  14.4 us (8%)
  other arithmetic  2.27 us (1%)
  between operations  2.06 us (1%)
    ppermute x1, starting transfers between devices, per_device(): wb = lax.ppermute(wa, 'modes', outer)  67.1 us
    all_to_all x1, blocking collectives, per_device(): lax.all_to_all(partial, 'modes', split_axis=0, concat_axis=0, tiled=True)  18.3 us
    dot_general x2, matrix products, turned(): out = jnp.dot(flat, onehot, preferred_element_type=jnp.float32)  14.7 us
    ppermute x1, waiting for transfers between devices, per_device(): wb = lax.ppermute(wa, 'modes', outer)  14.3 us
    convert_element_type x2, local copies, waits for them, and re-layouts, turned(): return out.astype(branch.dtype).reshape(branch.shape)  12.8 us
    pallas_call x1, Pallas kernels, per_device(): pl.pallas_call(two_branches, name='two_branches', out_shape=jax.ShapeDtyp...  11.1 us
    all_to_all x1, starting transfers between devices, per_device(): lax.all_to_all(cut, 'modes', split_axis=0, concat_axis=0, tiled=True)  7.52 us
    unnamed x10, local copies, waits for them, and re-layouts  4.39 us
  transfers between devices with their start and end apart: 5, of which 1 were waited for; matrix products, arithmetic and copies ran while one was open for 18% of the time, Pallas kernels for 6%

commit v1 on v0

--- a/solution.py
+++ b/solution.py
@@ -8,22 +8,46 @@
 TILES = 4
 
 
-def leg_index(order, leg_width):
-    positions = jnp.arange(leg_width, dtype=jnp.int32)
-    shifts = jnp.arange(order.shape[0], dtype=jnp.int32)
-    digits = jnp.right_shift(positions[:, None], shifts[None, :]) % 2
-    placed = jnp.left_shift(digits, order[None, :])
-    return jnp.sum(placed, axis=1)
-
-
-def turned(branch, order):
+def turn_columns(order, branch, out, onehot):
+    width = branch.shape[1]
+
+    @pl.when(pl.program_id(0) == 0)
+    def _():
+        positions = lax.broadcasted_iota(jnp.int32, (1, width), 1)
+        source = jnp.zeros((1, width), jnp.int32)
+        for bit in range(order.shape[0]):
+            source += jnp.left_shift(jnp.right_shift(positions, bit) & 1, order[bit])
+        rows = lax.broadcasted_iota(jnp.int32, (width, width), 0)
+        onehot[...] = jnp.where(rows == source, 1.0, 0.0).astype(onehot.dtype)
+
+    out[...] = jnp.dot(
+        branch[...], onehot[...], preferred_element_type=jnp.float32
+    ).astype(out.dtype)
+
+
+def turned(branch, order, name):
     width = branch.shape[2]
-    source = leg_index(order, width)
-    rows = lax.broadcasted_iota(jnp.int32, (width, width), 0)
-    onehot = (rows == source[None, :]).astype(branch.dtype)
     flat = branch.reshape(-1, width)
-    out = jnp.dot(flat, onehot, preferred_element_type=jnp.float32)
-    return out.astype(branch.dtype).reshape(branch.shape)
+    tile = flat.shape[0] // 8
+    out = pl.pallas_call(
+        turn_columns,
+        name=name,
+        grid=(8,),
+        out_shape=jax.ShapeDtypeStruct(flat.shape, flat.dtype),
+        in_specs=[
+            pl.BlockSpec(memory_space=pltpu.SMEM),
+            pl.BlockSpec((tile, width), lambda i: (i, 0)),
+        ],
+        out_specs=pl.BlockSpec((tile, width), lambda i: (i, 0)),
+        scratch_shapes=[pltpu.VMEM((width, width), flat.dtype)],
+        compiler_params=pltpu.CompilerParams(vmem_limit_bytes=58 * 2**20),
+        cost_estimate=pl.CostEstimate(
+            flops=2 * flat.shape[0] * width * width,
+            bytes_accessed=4 * flat.size,
+            transcendentals=0,
+        ),
+    )(order, flat)
+    return out.reshape(branch.shape)
 
 
 def complex_tile(w, values):
@@ -98,9 +122,6 @@
 
     cut = stem.reshape(2, entries, 2, 2, rest, 2, 2, 2, lanes)
     cut = cut.transpose(3, 7, 4, 5, 1, 0, 2, 6, 8).reshape(groups, entries, 8 * lanes)
-    arrived = lax.all_to_all(cut, "modes", split_axis=0, concat_axis=0, tiled=True)
-    x = arrived.reshape(groups * entries, 8 * lanes)
-
     pick = lax.dynamic_index_in_dim(slice_pick, me, 0, keepdims=False)
     own = lax.dynamic_index_in_dim(branch_three, pick, 0, keepdims=False)[:, 0]
     q = 2 * rest
@@ -111,14 +132,18 @@
     ]
     cores = [(i, i ^ 1) for i in range(groups)]
     crossed = lax.ppermute(own, "modes", middle)
+    w1 = turned(branch_one, leg_orders[0], "turn_one")
+    cut, crossed, w1, branch_two = lax.optimization_barrier((cut, crossed, w1, branch_two))
+    arrived = lax.all_to_all(cut, "modes", split_axis=0, concat_axis=0, tiled=True)
+    x = arrived.reshape(groups * entries, 8 * lanes)
+    w2 = turned(branch_two, leg_orders[1], "turn_two")
+    crossed, w2 = lax.optimization_barrier((crossed, w2))
     inner = (quarter == 1) | (quarter == 2)
     wa = jnp.where(inner, crossed, own)
     wb = lax.ppermute(wa, "modes", outer)
     wc = lax.ppermute(wa, "modes", cores)
     wd = lax.ppermute(wb, "modes", cores)
 
-    w1 = turned(branch_one, leg_orders[0])
-    w2 = turned(branch_two, leg_orders[1])
     width = w1.shape[1]
     half = width // 2
     any_spec = pl.BlockSpec(memory_space=pl.ANY)
@@ -136,7 +161,7 @@
             pltpu.VMEM((width, 8 * lanes), jnp.bfloat16),
             pltpu.SemaphoreType.DMA((1 + 2 * TILES,)),
         ],
-        compiler_params=pltpu.CompilerParams(vmem_limit_bytes=40 * 2**20),
+        compiler_params=pltpu.CompilerParams(vmem_limit_bytes=58 * 2**20),
         cost_estimate=pl.CostEstimate(
             flops=8 * width * width * 8 * lanes, bytes_accessed=12 * 2**20, transcendentals=0
         ),

time: 174 us -> 137 us (0.79)
  starting transfers between devices: 76.2 us -> 18.3 us
  waiting for transfers between devices: 14.4 us -> 46 us
  Pallas kernels: 15.3 us -> 36.6 us
  local copies, waits for them, and re-layouts: 29.9 us -> 13.7 us
  matrix products: 14.7 us -> 0 us
    ppermute x1, starting transfers between devices: 67.1 us -> 3.13 us  [per_device(): wb = lax.ppermute(wa, 'modes', outer)]
    ppermute x1, waiting for transfers between devices: 14.3 us -> 46 us  [per_device(): wb = lax.ppermute(wa, 'modes', outer)]
    pallas_call x0 -> x2, Pallas kernels: none -> 19.6 us  [turned(): pl.pallas_call(turn_columns, name=name, grid=(8,), out_shape=jax.ShapeDty...]
    dot_general x2 -> x0, matrix products: 14.7 us -> none  [turned(): out = jnp.dot(flat, onehot, preferred_element_type=jnp.float32)]
    convert_element_type x2 -> x0, local copies, waits for them, and re-layouts: 12.8 us -> none  [turned(): return out.astype(branch.dtype).reshape(branch.shape)]
    all_to_all x1, starting transfers between devices: 7.52 us -> 13.5 us  [per_device(): lax.all_to_all(cut, 'modes', split_axis=0, concat_axis=0, tiled=True)]
    unnamed x10 -> x8, local copies, waits for them, and re-layouts: 4.39 us -> 1.6 us
    pallas_call x1, Pallas kernels: 11.1 us -> 13.4 us  [per_device(): pl.pallas_call(two_branches, name='two_branches', out_shape=jax.ShapeDtyp...]
  transfers between devices with their start and end apart: 5 -> 5, of which waited for: 1 -> 1; matrix products, arithmetic and copies ran while one was open for 18% -> 6% of each run, Pallas kernels for 6% -> 24%
where the time goes in v1:
time: 137 us
  waiting for transfers between devices  46 us (34%)
  Pallas kernels  36.6 us (27%)
  blocking collectives  19.1 us (14%)
  starting transfers between devices  18.3 us (13%)
  local copies, waits for them, and re-layouts  13.7 us (10%)
  between operations  2.07 us (2%)
    ppermute x1, waiting for transfers between devices, per_device(): wb = lax.ppermute(wa, 'modes', outer)  46 us
    pallas_call x2, Pallas kernels, turned(): pl.pallas_call(turn_columns, name=name, grid=(8,), out_shape=jax.ShapeDty...  19.6 us
    all_to_all x1, blocking collectives, per_device(): lax.all_to_all(partial, 'modes', split_axis=0, concat_axis=0, tiled=True)  19.1 us
    all_to_all x1, starting transfers between devices, per_device(): lax.all_to_all(cut, 'modes', split_axis=0, concat_axis=0, tiled=True)  13.5 us
    pallas_call x1, Pallas kernels, per_device(): pl.pallas_call(two_branches, name='two_branches', out_shape=jax.ShapeDtyp...  13.4 us
    pallas_call x1, Pallas kernels, per_device(): pl.pallas_call(third_branch, name='third_branch', out_shape=jax.ShapeDtyp...  3.56 us
    ppermute x1, starting transfers between devices, per_device(): wb = lax.ppermute(wa, 'modes', outer)  3.13 us
    transpose x1, local copies, waits for them, and re-layouts, per_device(): cut.transpose(3, 7, 4, 5, 1, 0, 2, 6, 8).reshape(groups, entries, 8 * lanes)  3.07 us
  transfers between devices with their start and end apart: 5, of which 1 were waited for; matrix products, arithmetic and copies ran while one was open for 6% of the time, Pallas kernels for 24%

profile of v1, /device:TPU:0, one launch (start us, length us, event | category | flops | bytes accessed | tf_op | source)
XLA Modules:
  0.0 136.7 jit_solution(2437138684387349122)
XLA Ops:
  0.0 0.0 copy-start.2
  0.0 1.4 %dynamic_slice.8 = s32[1]{0:T(128)} dynamic-slice(s32[16]{0:T(128)} %param.11, s32[]{:T(128)S(6)} %select_n.36), dynamic_slice_sizes={1} | dynamic-slice | bytes 12 | tf_op jit(solution)/shard_map/jit(dynamic_index_in_dim)/dynamic_slice | solution.py:125
  3.3 1.3 dynamic-slice_bitcast_fusion
  4.6 1.7 %collective-permute-start = (bf16[2,512,512]{2,1,0:T(8,128)(2,1)S(1)}, bf16[2,512,512]{2,1,0:T(8,128)(2,1)}, u32[]{:S(2)}, u32[]{:S(2)}) collective-permute-start(bf16[2,512,512]{2,1,0:T(8,128)(2,1)S(1)} %dynamic-slice_bitcast_fusion), channel_id=1, source_target_pairs={{4,8},{5,9},{6,10},{7,11},{8,4},{9,5},{10,6},{11,7},{20,24},{21,25... | collective-permute-start | bytes 3145736 | tf_op jit(solution)/shard_map/ppermute | solution.py:134
  6.3 0.0 copy-done.2
  6.3 2.1 %reshape.31 = bf16[2,64,2,2,2,2,2,2,128]{8,7,6,5,4,3,2,1,0:T(2,128)(2,1)} reshape(bf16[2,1,64,32,256]{4,3,2,1,0:T(8,128)(2,1)S(1)} %copy-done.2) | data formatting | bytes 4194304 | tf_op jit(solution)/shard_map/reshape | solution.py:123
  8.4 3.1 %copy.9 = bf16[2,2,2,2,64,2,2,2,128]{8,7,6,5,4,3,2,1,0:T(2,128)(2,1)S(1)} copy(bf16[2,2,2,2,64,2,2,2,128]{8,1,7,3,2,0,6,4,5:T(2,128)(2,1)} %bitcast.22) | data formatting | bytes 4194304 | tf_op jit(solution)/shard_map/transpose | solution.py:124
  11.5 0.0 copy-start.3
  11.5 2.8 %reshape.32 = bf16[16,64,1024]{2,1,0:T(8,128)(2,1)} reshape(bf16[2,2,2,2,64,2,2,2,128]{8,7,6,5,4,3,2,1,0:T(2,128)(2,1)S(1)} %copy.9) | data formatting | bytes 4194304 | tf_op jit(solution)/shard_map/reshape | solution.py:124
  14.3 0.0 copy-done.3
  14.3 0.5 slice_bitcast_fusion
  14.8 9.7 %turn_one.1 = bf16[2048,1024]{1,0:T(8,128)(2,1)} custom-call(s32[10]{0:T(128)} %get-tuple-element.18.order, bf16[2048,1024]{1,0:T(8,128)(2,1)} %bitcast.24), custom_call_target="tpu_custom_call" | custom-call | flops 4294967296 | bytes 8388608 | tf_op jit(solution)/shard_map/turn_one/pallas_call | solution.py:32
  24.5 0.0 collective-permute-done
  24.5 13.5 %all-to-all-start = ((bf16[16,64,1024]{2,1,0:T(8,128)(2,1)}), bf16[16,64,1024]{2,1,0:T(8,128)(2,1)}, u32[]{:S(2)}, u32[]{:S(2)}) async-start(bf16[16,64,1024]{2,1,0:T(8,128)(2,1)} %reshape.32), calls=%async_computation | async-start | bytes 4194304 | tf_op jit(solution)/shard_map/all_to_all | solution.py:137
  38.0 0.0 copy-start.1
  38.0 9.9 %turn_two.1 = bf16[2048,1024]{1,0:T(8,128)(2,1)} custom-call(s32[10]{0:T(128)} %get-tuple-element.17.order, bf16[2048,1024]{1,0:T(8,128)(2,1)} %bitcast.25), custom_call_target="tpu_custom_call" | custom-call | flops 4294967296 | bytes 8388608 | tf_op jit(solution)/shard_map/turn_two/pallas_call | solution.py:32
  47.9 0.0 copy-done.1
  47.9 0.1 broadcast_select_fusion.wa
  48.1 3.1 %collective-permute-start.1 = (bf16[2,512,512]{2,1,0:T(8,128)(2,1)S(1)}, bf16[2,512,512]{2,1,0:T(8,128)(2,1)S(1)}, u32[]{:S(2)}, u32[]{:S(2)}) collective-permute-start(bf16[2,512,512]{2,1,0:T(8,128)(2,1)S(1)} %broadcast_select_fusion.wa), channel_id=1, source_target_pairs={{0,4},{1,5},{2,6},{3,7},{4,0},{5,1},{6,2},{7,3},{8,12},{9,13},{10,... | collective-permute-start | bytes 3145736 | tf_op jit(solution)/shard_map/ppermute | solution.py:143
  51.2 0.0 collective-permute-start.2
  51.2 46.0 %collective-permute-done.1.wb = bf16[2,512,512]{2,1,0:T(8,128)(2,1)S(1)} collective-permute-done((bf16[2,512,512]{2,1,0:T(8,128)(2,1)S(1)}, bf16[2,512,512]{2,1,0:T(8,128)(2,1)S(1)}, u32[]{:S(2)}, u32[]{:S(2)}) %collective-permute-start.1) | collective-permute-done | bytes 1048608 | tf_op jit(solution)/shard_map/ppermute | solution.py:143
  97.2 0.0 collective-permute-start.3
  97.2 0.1 pad_add_fusion.place
  97.3 0.0 all-to-all-done
  97.3 13.4 %two_branches.1.values = bf16[4,512,512]{2,1,0:T(8,128)(2,1)} custom-call(bf16[1024,1024]{1,0:T(8,128)(2,1)} %bitcast.11.x_hbm, bf16[2,1024,1024]{2,1,0:T(8,128)(2,1)} %bitcast.26, bf16[2,1024,1024]{2,1,0:T(8,128)(2,1)} %bitcast.27), custom_call_target="tpu_custom_call" | custom-call | flops 8589934592 | bytes 12582912 | tf_op jit(solution)/shard_map/two_branches/pallas_call | solution.py:151
  110.7 0.0 collective-permute-done.2.wc
  110.7 0.0 collective-permute-done.3.wd
  110.7 0.0 copy-start
  110.7 1.6 %copy-done = bf16[4,512,512]{2,1,0:T(8,128)(2,1)S(1)} copy-done((bf16[4,512,512]{2,1,0:T(8,128)(2,1)S(1)}, bf16[4,512,512]{2,1,0:T(8,128)(2,1)}, u32[]{:S(2)}) %copy-start) | copy-done | bytes 2097176
  112.3 3.6 %third_branch.1 = bf16[512,512]{1,0:T(8,128)(2,1)S(1)} custom-call(s32[2]{0:T(128)S(1)} %pad_add_fusion.place, bf16[2,512,512]{2,1,0:T(8,128)(2,1)S(1)} %broadcast_select_fusion.wa, bf16[2,512,512]{2,1,0:T(8,128)(2,1)S(1)} %collective-permute-done.1.wb, bf16[2,512,512]{2,1,0:T(8,128)(2,1)S(1)} %collective-permute-done.2.wc, ...), custom_call_target="tpu_custom_call" | custom-call | flops 2147483648 | bytes 7340032 | tf_op jit(solution)/shard_map/third_branch/pallas_call | solution.py:171
  115.8 19.1 %all_to_all.14 = bf16[16,32,512]{2,1,0:T(8,128)(2,1)S(1)} all-to-all(bf16[16,32,512]{2,1,0:T(8,128)(2,1)S(1)} %bitcast.21), channel_id=1, replica_groups=mesh['parts'=2,'modes'=16] {'modes'}, dimensions={0} | all-to-all | bytes 1048576 | tf_op jit(solution)/shard_map/all_to_all | solution.py:183
  135.0 0.1 reshape.38
  135.1 0.8 reduce_sum.12
  135.9 0.1 copy.12
  136.0 0.7 reshape.40
Async XLA Ops:
  0.0 6.3 %copy-start.2 = (bf16[2,1,64,32,256]{4,3,2,1,0:T(8,128)(2,1)S(1)}, bf16[2,1,64,32,256]{4,3,2,1,0:T(8,128)(2,1)}, u32[]{:S(2)}) copy-start(bf16[2,1,64,32,256]{4,3,2,1,0:T(8,128)(2,1)} %param.6) | copy-start | bytes 6291460
  4.6 19.9 %collective-permute-start = (bf16[2,512,512]{2,1,0:T(8,128)(2,1)S(1)}, bf16[2,512,512]{2,1,0:T(8,128)(2,1)}, u32[]{:S(2)}, u32[]{:S(2)}) collective-permute-start(bf16[2,512,512]{2,1,0:T(8,128)(2,1)S(1)} %dynamic-slice_bitcast_fusion), channel_id=1, source_target_pairs={{4,8},{5,9},{6,10},{7,11},{8,4},{9,5},{10,6},{11,7},{20,24},{21,25... | collective-permute-start | bytes 3145736 | tf_op jit(solution)/shard_map/ppermute | solution.py:134
  11.5 2.8 %copy-start.3 = (s32[2,10]{1,0:T(2,128)S(1)}, s32[2,10]{1,0:T(2,128)}, u32[]{:S(2)}) copy-start(s32[2,10]{1,0:T(2,128)} %param.10) | copy-start | bytes 244
  24.5 72.8 %all-to-all-start = ((bf16[16,64,1024]{2,1,0:T(8,128)(2,1)}), bf16[16,64,1024]{2,1,0:T(8,128)(2,1)}, u32[]{:S(2)}, u32[]{:S(2)}) async-start(bf16[16,64,1024]{2,1,0:T(8,128)(2,1)} %reshape.32), calls=%async_computation | async-start | bytes 4194304 | tf_op jit(solution)/shard_map/all_to_all | solution.py:137
  38.0 9.9 %copy-start.1 = (bf16[2,2,1,512,512]{4,3,2,1,0:T(8,128)(2,1)S(1)}, bf16[2,2,1,512,512]{4,3,2,1,0:T(8,128)(2,1)}, u32[]{:S(2)}) copy-start(bf16[2,2,1,512,512]{4,3,2,1,0:T(8,128)(2,1)} %param.9) | copy-start | bytes 6291460
  48.1 49.1 %collective-permute-start.1 = (bf16[2,512,512]{2,1,0:T(8,128)(2,1)S(1)}, bf16[2,512,512]{2,1,0:T(8,128)(2,1)S(1)}, u32[]{:S(2)}, u32[]{:S(2)}) collective-permute-start(bf16[2,512,512]{2,1,0:T(8,128)(2,1)S(1)} %broadcast_select_fusion.wa), channel_id=1, source_target_pairs={{0,4},{1,5},{2,6},{3,7},{4,0},{5,1},{6,2},{7,3},{8,12},{9,13},{10,... | collective-permute-start | bytes 3145736 | tf_op jit(solution)/shard_map/ppermute | solution.py:143
  51.2 59.5 %collective-permute-start.2 = (bf16[2,512,512]{2,1,0:T(8,128)(2,1)S(1)}, bf16[2,512,512]{2,1,0:T(8,128)(2,1)S(1)}, u32[]{:S(2)}, u32[]{:S(2)}) collective-permute-start(bf16[2,512,512]{2,1,0:T(8,128)(2,1)S(1)} %broadcast_select_fusion.wa), channel_id=1, source_target_pairs={{0,1},{1,0},{2,3},{3,2},{4,5},{5,4},{6,7},{7,6},{8,9},{9,8},{10,11... | collective-permute-start | bytes 3145736 | tf_op jit(solution)/shard_map/ppermute | solution.py:144
  97.2 13.5 %collective-permute-start.3 = (bf16[2,512,512]{2,1,0:T(8,128)(2,1)S(1)}, bf16[2,512,512]{2,1,0:T(8,128)(2,1)}, u32[]{:S(2)}, u32[]{:S(2)}) collective-permute-start(bf16[2,512,512]{2,1,0:T(8,128)(2,1)S(1)} %collective-permute-done.1.wb), channel_id=1, source_target_pairs={{0,1},{1,0},{2,3},{3,2},{4,5},{5,4},{6,7},{7,6},{8,9},{9,8},{10,11... | collective-permute-start | bytes 3145736 | tf_op jit(solution)/shard_map/ppermute | solution.py:145
  110.7 1.6 %copy-start = (bf16[4,512,512]{2,1,0:T(8,128)(2,1)S(1)}, bf16[4,512,512]{2,1,0:T(8,128)(2,1)}, u32[]{:S(2)}) copy-start(bf16[4,512,512]{2,1,0:T(8,128)(2,1)} %two_branches.1.values) | copy-start | bytes 6291460

commit v2 on v1

--- a/solution.py
+++ b/solution.py
@@ -96,15 +96,21 @@
                 out[td, c : c + tile, at : at + lanes] = parts[r][:, td * lanes : (td + 1) * lanes]
 
 
-def third_branch(place, wa, wb, wc, wd, values, out):
+def third_branch(place, ar, ai, br, bi, cr, ci, dr, di, values, out):
     k2 = place[0]
     k0 = place[1]
     half = values.shape[2] // 2
     p = q = None
-    for w, t, d in ((wa, k2, k0), (wb, 1 - k2, k0), (wc, k2, 1 - k0), (wd, 1 - k2, 1 - k0)):
+    sources = (
+        (ar, ai, k2, k0),
+        (br, bi, 1 - k2, k0),
+        (cr, ci, k2, 1 - k0),
+        (dr, di, 1 - k2, 1 - k0),
+    )
+    for real, imag, t, d in sources:
         block = values[2 * t + d]
-        pp = jnp.dot(w[0], block, preferred_element_type=jnp.float32)
-        qq = jnp.dot(w[1], block, preferred_element_type=jnp.float32)
+        pp = jnp.dot(real[...], block, preferred_element_type=jnp.float32)
+        qq = jnp.dot(imag[...], block, preferred_element_type=jnp.float32)
         p = pp if p is None else p + pp
         q = qq if q is None else q + qq
     out[:, :half] = (p[:, :half] - q[:, half:]).astype(out.dtype)
@@ -131,18 +137,24 @@
         (i, i + q if (i // q) % 2 == 0 else i - q) for i in range(groups)
     ]
     cores = [(i, i ^ 1) for i in range(groups)]
-    crossed = lax.ppermute(own, "modes", middle)
+    inner = (quarter == 1) | (quarter == 2)
+    crossed_real = lax.ppermute(own[0], "modes", middle)
+    wa_real = jnp.where(inner, crossed_real, own[0])
+    wb_real = lax.ppermute(wa_real, "modes", outer)
+    crossed = lax.ppermute(own[1], "modes", middle)
     w1 = turned(branch_one, leg_orders[0], "turn_one")
     cut, crossed, w1, branch_two = lax.optimization_barrier((cut, crossed, w1, branch_two))
     arrived = lax.all_to_all(cut, "modes", split_axis=0, concat_axis=0, tiled=True)
     x = arrived.reshape(groups * entries, 8 * lanes)
     w2 = turned(branch_two, leg_orders[1], "turn_two")
     crossed, w2 = lax.optimization_barrier((crossed, w2))
-    inner = (quarter == 1) | (quarter == 2)
-    wa = jnp.where(inner, crossed, own)
-    wb = lax.ppermute(wa, "modes", outer)
-    wc = lax.ppermute(wa, "modes", cores)
-    wd = lax.ppermute(wb, "modes", cores)
+    wa_imag = jnp.where(inner, crossed, own[1])
+    wb_imag = lax.ppermute(wa_imag, "modes", outer)
+    wc_real = lax.ppermute(wa_real, "modes", cores)
+    wc_imag = lax.ppermute(wa_imag, "modes", cores)
+    wd_real = lax.ppermute(wb_real, "modes", cores)
+    wd_imag = lax.ppermute(wb_imag, "modes", cores)
+    blocks = (wa_real, wa_imag, wb_real, wb_imag, wc_real, wc_imag, wd_real, wd_imag)
 
     width = w1.shape[1]
     half = width // 2
@@ -172,13 +184,13 @@
         third_branch,
         name="third_branch",
         out_shape=jax.ShapeDtypeStruct((out_width, 4 * lanes), jnp.bfloat16),
-        in_specs=[pl.BlockSpec(memory_space=pltpu.SMEM)] + [vmem] * 5,
+        in_specs=[pl.BlockSpec(memory_space=pltpu.SMEM)] + [vmem] * 9,
         out_specs=vmem,
         compiler_params=pltpu.CompilerParams(vmem_limit_bytes=24 * 2**20),
         cost_estimate=pl.CostEstimate(
             flops=16 * out_width * half * 4 * lanes, bytes_accessed=7 * 2**20, transcendentals=0
         ),
-    )(jnp.stack([k2, k0]).astype(jnp.int32), wa, wb, wc, wd, values)
+    )(jnp.stack([k2, k0]).astype(jnp.int32), *blocks, values)
 
     pieces = lax.all_to_all(partial, "modes", split_axis=0, concat_axis=0, tiled=True)
     mine = out_width // groups

time: 137 us -> 144 us (1.051)
  starting transfers between devices: 18.3 us -> 60.5 us
  waiting for transfers between devices: 46 us -> 11 us
    ppermute x4 -> x8, starting transfers between devices: 4.83 us -> 53.1 us  [the longest x1 44.5 us: per_device(): wb_real = lax.ppermute(wa_real, 'modes', outer)]
    ppermute x4 -> x8, waiting for transfers between devices: 46 us -> 11 us  [the longest x1 11 us: per_device(): wb_real = lax.ppermute(wa_real, 'modes', outer)]
    all_to_all x1, starting transfers between devices: 13.5 us -> 7.44 us  [per_device(): lax.all_to_all(cut, 'modes', split_axis=0, concat_axis=0, tiled=True)]
  transfers between devices with their start and end apart: 5 -> 9, of which waited for: 1 -> 1; matrix products, arithmetic and copies ran while one was open for 6% -> 6% of each run, Pallas kernels for 24% -> 23%
where the time goes in v2:
time: 144 us; the launch traced here: 143 us
  starting transfers between devices  60.5 us (42%)
  Pallas kernels  36.4 us (25%)
  blocking collectives  18.2 us (13%)
  local copies, waits for them, and re-layouts  13.7 us (10%)
  waiting for transfers between devices  11 us (8%)
  between operations  2.1 us (1%)
    ppermute x1, starting transfers between devices, per_device(): wb_real = lax.ppermute(wa_real, 'modes', outer)  44.5 us
    pallas_call x2, Pallas kernels, turned(): pl.pallas_call(turn_columns, name=name, grid=(8,), out_shape=jax.ShapeDty...  19.5 us
    all_to_all x1, blocking collectives, per_device(): lax.all_to_all(partial, 'modes', split_axis=0, concat_axis=0, tiled=True)  18.2 us
    pallas_call x1, Pallas kernels, per_device(): pl.pallas_call(two_branches, name='two_branches', out_shape=jax.ShapeDtyp...  13.4 us
    ppermute x1, waiting for transfers between devices, per_device(): wb_real = lax.ppermute(wa_real, 'modes', outer)  11 us
    all_to_all x1, starting transfers between devices, per_device(): lax.all_to_all(cut, 'modes', split_axis=0, concat_axis=0, tiled=True)  7.44 us
    ppermute x1, starting transfers between devices, per_device(): wb_imag = lax.ppermute(wa_imag, 'modes', outer)  5.65 us
    pallas_call x1, Pallas kernels, per_device(): pl.pallas_call(third_branch, name='third_branch', out_shape=jax.ShapeDtyp...  3.54 us
  transfers between devices with their start and end apart: 9, of which 1 were waited for; matrix products, arithmetic and copies ran while one was open for 6% of the time, Pallas kernels for 23%

profile of v2, /device:TPU:0, one launch (start us, length us, event | category | flops | bytes accessed | tf_op | source)
XLA Modules:
  0.0 142.9 jit_solution(13029941082595156668)
XLA Ops:
  0.0 0.0 copy-start.1
  0.0 1.4 dynamic_slice.8
  3.3 1.3 dynamic-slice_bitcast_fusion
  4.6 1.5 %collective-permute-start.1 = (bf16[512,512]{1,0:T(8,128)(2,1)S(1)}, bf16[512,512]{1,0:T(8,128)(2,1)}, u32[]{:S(2)}, u32[]{:S(2)}) collective-permute-start(bf16[512,512]{1,0:T(8,128)(2,1)S(1)} %get-tuple-element.17), channel_id=1, source_target_pairs={{4,8},{5,9},{6,10},{7,11},{8,4},{9,5},{10,6},{11,7},{20,24},{21,25... | collective-permute-start | bytes 1572872 | tf_op jit(solution)/shard_map/ppermute | solution.py:144
  6.1 0.0 copy-done.1
  6.1 2.1 %reshape.35 = bf16[2,64,2,2,2,2,2,2,128]{8,7,6,5,4,3,2,1,0:T(2,128)(2,1)} reshape(bf16[2,1,64,32,256]{4,3,2,1,0:T(8,128)(2,1)S(1)} %copy-done.1) | data formatting | bytes 4194304 | tf_op jit(solution)/shard_map/reshape | solution.py:129
  8.2 3.1 %copy.9 = bf16[2,2,2,2,64,2,2,2,128]{8,7,6,5,4,3,2,1,0:T(2,128)(2,1)S(1)} copy(bf16[2,2,2,2,64,2,2,2,128]{8,1,7,3,2,0,6,4,5:T(2,128)(2,1)} %bitcast.22) | data formatting | bytes 4194304 | tf_op jit(solution)/shard_map/transpose | solution.py:130
  11.2 0.0 copy-start.2
  11.2 2.8 %reshape.36 = bf16[16,64,1024]{2,1,0:T(8,128)(2,1)} reshape(bf16[2,2,2,2,64,2,2,2,128]{8,7,6,5,4,3,2,1,0:T(2,128)(2,1)S(1)} %copy.9) | data formatting | bytes 4194304 | tf_op jit(solution)/shard_map/reshape | solution.py:130
  14.0 0.0 copy-done.2
  14.0 0.5 slice_bitcast_fusion
  14.5 9.7 %turn_one.1 = bf16[2048,1024]{1,0:T(8,128)(2,1)} custom-call(s32[10]{0:T(128)} %get-tuple-element.20.order, bf16[2048,1024]{1,0:T(8,128)(2,1)} %bitcast.24), custom_call_target="tpu_custom_call" | custom-call | flops 4294967296 | bytes 8388608 | tf_op jit(solution)/shard_map/turn_one/pallas_call | solution.py:32
  24.3 0.0 collective-permute-done.1
  24.3 7.4 %all-to-all-start = ((bf16[16,64,1024]{2,1,0:T(8,128)(2,1)}), bf16[16,64,1024]{2,1,0:T(8,128)(2,1)}, u32[]{:S(2)}, u32[]{:S(2)}) async-start(bf16[16,64,1024]{2,1,0:T(8,128)(2,1)} %reshape.36), calls=%async_computation | async-start | bytes 4194304 | tf_op jit(solution)/shard_map/all_to_all | solution.py:147
  31.7 0.9 collective-permute-start
  32.6 9.8 %turn_two.1 = bf16[2048,1024]{1,0:T(8,128)(2,1)} custom-call(s32[10]{0:T(128)} %get-tuple-element.19.order, bf16[2048,1024]{1,0:T(8,128)(2,1)} %bitcast.25), custom_call_target="tpu_custom_call" | custom-call | flops 4294967296 | bytes 8388608 | tf_op jit(solution)/shard_map/turn_two/pallas_call | solution.py:32
  42.4 0.1 broadcast_select_fusion.ai
  42.4 5.6 %collective-permute-start.3 = (bf16[512,512]{1,0:T(8,128)(2,1)S(1)}, bf16[512,512]{1,0:T(8,128)(2,1)S(1)}, u32[]{:S(2)}, u32[]{:S(2)}) collective-permute-start(bf16[512,512]{1,0:T(8,128)(2,1)S(1)} %broadcast_select_fusion.ai), channel_id=1, source_target_pairs={{0,4},{1,5},{2,6},{3,7},{4,0},{5,1},{6,2},{7,3},{8,12},{9,13},{10,... | collective-permute-start | bytes 1572872 | tf_op jit(solution)/shard_map/ppermute | solution.py:152
  48.1 0.0 collective-permute-done
  48.1 0.1 broadcast_select_fusion.1.ar
  48.2 44.5 %collective-permute-start.2 = (bf16[512,512]{1,0:T(8,128)(2,1)S(1)}, bf16[512,512]{1,0:T(8,128)(2,1)S(1)}, u32[]{:S(2)}, u32[]{:S(2)}) collective-permute-start(bf16[512,512]{1,0:T(8,128)(2,1)S(1)} %broadcast_select_fusion.1.ar), channel_id=1, source_target_pairs={{0,4},{1,5},{2,6},{3,7},{4,0},{5,1},{6,2},{7,3},{8,12},{9,13},{10,... | collective-permute-start | bytes 1572872 | tf_op jit(solution)/shard_map/ppermute | solution.py:143
  92.7 0.1 pad_add_fusion.place
  92.7 0.0 collective-permute-start.5
  92.7 0.5 collective-permute-start.4
  93.2 0.0 collective-permute-done.3.bi
  93.2 0.1 collective-permute-start.7
  93.3 11.0 %collective-permute-done.2.br = bf16[512,512]{1,0:T(8,128)(2,1)S(1)} collective-permute-done((bf16[512,512]{1,0:T(8,128)(2,1)S(1)}, bf16[512,512]{1,0:T(8,128)(2,1)S(1)}, u32[]{:S(2)}, u32[]{:S(2)}) %collective-permute-start.2) | collective-permute-done | bytes 524320 | tf_op jit(solution)/shard_map/ppermute | solution.py:143
  104.3 0.0 collective-permute-start.6
  104.3 0.0 all-to-all-done
  104.3 13.4 %two_branches.1.values = bf16[4,512,512]{2,1,0:T(8,128)(2,1)} custom-call(bf16[1024,1024]{1,0:T(8,128)(2,1)} %bitcast.12.x_hbm, bf16[2,1024,1024]{2,1,0:T(8,128)(2,1)} %bitcast.26, bf16[2,1024,1024]{2,1,0:T(8,128)(2,1)} %bitcast.27), custom_call_target="tpu_custom_call" | custom-call | flops 8589934592 | bytes 12582912 | tf_op jit(solution)/shard_map/two_branches/pallas_call | solution.py:163
  117.7 0.0 collective-permute-done.5.ci
  117.7 0.0 collective-permute-done.4.cr
  117.7 0.0 collective-permute-done.7.di
  117.7 0.0 collective-permute-done.6.dr
  117.7 0.0 copy-start
  117.7 1.6 %copy-done = bf16[4,512,512]{2,1,0:T(8,128)(2,1)S(1)} copy-done((bf16[4,512,512]{2,1,0:T(8,128)(2,1)S(1)}, bf16[4,512,512]{2,1,0:T(8,128)(2,1)}, u32[]{:S(2)}) %copy-start) | copy-done | bytes 2097176
  119.3 3.5 %third_branch.1 = bf16[512,512]{1,0:T(8,128)(2,1)S(1)} custom-call(s32[2]{0:T(128)S(1)} %pad_add_fusion.place, bf16[512,512]{1,0:T(8,128)(2,1)S(1)} %broadcast_select_fusion.1.ar, bf16[512,512]{1,0:T(8,128)(2,1)S(1)} %broadcast_select_fusion.ai, bf16[512,512]{1,0:T(8,128)(2,1)S(1)} %collective-permute-done.2.br, ...), custom_call_target="tpu_custom_call" | custom-call | flops 2147483648 | bytes 7340032 | tf_op jit(solution)/shard_map/third_branch/pallas_call | solution.py:183
  122.9 18.2 %all_to_all.14 = bf16[16,32,512]{2,1,0:T(8,128)(2,1)S(1)} all-to-all(bf16[16,32,512]{2,1,0:T(8,128)(2,1)S(1)} %bitcast.21), channel_id=1, replica_groups=mesh['parts'=2,'modes'=16] {'modes'}, dimensions={0} | all-to-all | bytes 1048576 | tf_op jit(solution)/shard_map/all_to_all | solution.py:195
  141.1 0.1 reshape.42
  141.2 0.8 reduce_sum.12
  142.0 0.1 copy.12
  142.1 0.7 reshape.44
Async XLA Ops:
  0.0 6.1 %copy-start.1 = (bf16[2,1,64,32,256]{4,3,2,1,0:T(8,128)(2,1)S(1)}, bf16[2,1,64,32,256]{4,3,2,1,0:T(8,128)(2,1)}, u32[]{:S(2)}) copy-start(bf16[2,1,64,32,256]{4,3,2,1,0:T(8,128)(2,1)} %param.6) | copy-start | bytes 6291460
  4.6 19.6 %collective-permute-start.1 = (bf16[512,512]{1,0:T(8,128)(2,1)S(1)}, bf16[512,512]{1,0:T(8,128)(2,1)}, u32[]{:S(2)}, u32[]{:S(2)}) collective-permute-start(bf16[512,512]{1,0:T(8,128)(2,1)S(1)} %get-tuple-element.17), channel_id=1, source_target_pairs={{4,8},{5,9},{6,10},{7,11},{8,4},{9,5},{10,6},{11,7},{20,24},{21,25... | collective-permute-start | bytes 1572872 | tf_op jit(solution)/shard_map/ppermute | solution.py:144
  11.2 2.8 %copy-start.2 = (s32[2,10]{1,0:T(2,128)S(1)}, s32[2,10]{1,0:T(2,128)}, u32[]{:S(2)}) copy-start(s32[2,10]{1,0:T(2,128)} %param.10) | copy-start | bytes 244
  24.3 80.0 %all-to-all-start = ((bf16[16,64,1024]{2,1,0:T(8,128)(2,1)}), bf16[16,64,1024]{2,1,0:T(8,128)(2,1)}, u32[]{:S(2)}, u32[]{:S(2)}) async-start(bf16[16,64,1024]{2,1,0:T(8,128)(2,1)} %reshape.36), calls=%async_computation | async-start | bytes 4194304 | tf_op jit(solution)/shard_map/all_to_all | solution.py:147
  31.7 16.4 %collective-permute-start = (bf16[512,512]{1,0:T(8,128)(2,1)S(1)}, bf16[512,512]{1,0:T(8,128)(2,1)S(1)}, u32[]{:S(2)}, u32[]{:S(2)}) collective-permute-start(bf16[512,512]{1,0:T(8,128)(2,1)S(1)} %get-tuple-element.18), channel_id=1, source_target_pairs={{4,8},{5,9},{6,10},{7,11},{8,4},{9,5},{10,6},{11,7},{20,24},{21,25... | collective-permute-start | bytes 1572872 | tf_op jit(solution)/shard_map/ppermute | solution.py:141
  42.4 50.8 %collective-permute-start.3 = (bf16[512,512]{1,0:T(8,128)(2,1)S(1)}, bf16[512,512]{1,0:T(8,128)(2,1)S(1)}, u32[]{:S(2)}, u32[]{:S(2)}) collective-permute-start(bf16[512,512]{1,0:T(8,128)(2,1)S(1)} %broadcast_select_fusion.ai), channel_id=1, source_target_pairs={{0,4},{1,5},{2,6},{3,7},{4,0},{5,1},{6,2},{7,3},{8,12},{9,13},{10,... | collective-permute-start | bytes 1572872 | tf_op jit(solution)/shard_map/ppermute | solution.py:152
  48.2 56.1 %collective-permute-start.2 = (bf16[512,512]{1,0:T(8,128)(2,1)S(1)}, bf16[512,512]{1,0:T(8,128)(2,1)S(1)}, u32[]{:S(2)}, u32[]{:S(2)}) collective-permute-start(bf16[512,512]{1,0:T(8,128)(2,1)S(1)} %broadcast_select_fusion.1.ar), channel_id=1, source_target_pairs={{0,4},{1,5},{2,6},{3,7},{4,0},{5,1},{6,2},{7,3},{8,12},{9,13},{10,... | collective-permute-start | bytes 1572872 | tf_op jit(solution)/shard_map/ppermute | solution.py:143
  92.7 25.0 %collective-permute-start.5 = (bf16[512,512]{1,0:T(8,128)(2,1)S(1)}, bf16[512,512]{1,0:T(8,128)(2,1)S(1)}, u32[]{:S(2)}, u32[]{:S(2)}) collective-permute-start(bf16[512,512]{1,0:T(8,128)(2,1)S(1)} %broadcast_select_fusion.ai), channel_id=1, source_target_pairs={{0,1},{1,0},{2,3},{3,2},{4,5},{5,4},{6,7},{7,6},{8,9},{9,8},{10,11... | collective-permute-start | bytes 1572872 | tf_op jit(solution)/shard_map/ppermute | solution.py:154
  92.7 25.0 %collective-permute-start.4 = (bf16[512,512]{1,0:T(8,128)(2,1)S(1)}, bf16[512,512]{1,0:T(8,128)(2,1)S(1)}, u32[]{:S(2)}, u32[]{:S(2)}) collective-permute-start(bf16[512,512]{1,0:T(8,128)(2,1)S(1)} %broadcast_select_fusion.1.ar), channel_id=1, source_target_pairs={{0,1},{1,0},{2,3},{3,2},{4,5},{5,4},{6,7},{7,6},{8,9},{9,8},{10,11... | collective-permute-start | bytes 1572872 | tf_op jit(solution)/shard_map/ppermute | solution.py:153
  93.2 24.5 %collective-permute-start.7 = (bf16[512,512]{1,0:T(8,128)(2,1)S(1)}, bf16[512,512]{1,0:T(8,128)(2,1)}, u32[]{:S(2)}, u32[]{:S(2)}) collective-permute-start(bf16[512,512]{1,0:T(8,128)(2,1)S(1)} %collective-permute-done.3.bi), channel_id=1, source_target_pairs={{0,1},{1,0},{2,3},{3,2},{4,5},{5,4},{6,7},{7,6},{8,9},{9,8},{10,11... | collective-permute-start | bytes 1572872 | tf_op jit(solution)/shard_map/ppermute | solution.py:156
  104.3 13.4 %collective-permute-start.6 = (bf16[512,512]{1,0:T(8,128)(2,1)S(1)}, bf16[512,512]{1,0:T(8,128)(2,1)}, u32[]{:S(2)}, u32[]{:S(2)}) collective-permute-start(bf16[512,512]{1,0:T(8,128)(2,1)S(1)} %collective-permute-done.2.br), channel_id=1, source_target_pairs={{0,1},{1,0},{2,3},{3,2},{4,5},{5,4},{6,7},{7,6},{8,9},{9,8},{10,11... | collective-permute-start | bytes 1572872 | tf_op jit(solution)/shard_map/ppermute | solution.py:155
  117.7 1.6 %copy-start = (bf16[4,512,512]{2,1,0:T(8,128)(2,1)S(1)}, bf16[4,512,512]{2,1,0:T(8,128)(2,1)}, u32[]{:S(2)}) copy-start(bf16[4,512,512]{2,1,0:T(8,128)(2,1)} %two_branches.1.values) | copy-start | bytes 6291460
